TPU v7x, 16 devices: a 4x2x1 block of a 4x4x8 slice. The times are simulated.
16 devices in a mesh: dp: 2 (over y, z), sp: 8 (over x, core).
Axes of the slice: x: 4, y: 2, z: 1, core: 2. Of those that a mesh axis runs over, the one named last changes fastest.
The devices are a block of a 4x4x8 slice.
Arguments:
- hidden: bfloat16 [256, 4544], P('dp'), parts along dimension 0
- ln_gamma: float32 [4544], replicated
- ln_beta: float32 [4544], replicated
- w_qkv: bfloat16 [4544, 4672], replicated
- w_out: bfloat16 [4544, 4544], replicated
- w_up: bfloat16 [4544, 18176], P(None, 'sp')
- w_down: bfloat16 [18176, 4544], P('sp')
- k_cache: bfloat16 [256, 8192, 64], P('dp', 'sp'), parts along dimension 0
- v_cache: bfloat16 [256, 8192, 64], P('dp', 'sp'), parts along dimension 0
- positions: int32 [256], P('dp'), parts along dimension 0
Outputs:
- output 1: bfloat16 [256, 4544], P('dp'), parts along dimension 0
- output 2: bfloat16 [256, 8192, 64], P('dp', 'sp'), parts along dimension 0
- output 3: bfloat16 [256, 8192, 64], P('dp', 'sp'), parts along dimension 0
There are 2 independent parts. A program takes and returns all parts, laid end to end along the dimension named above; an argument that names none is the same for every part.
All inputs are finite; a program needn't handle non-finite values.
Results may differ from a plain program's by a relative error of at most 0.00624681.
Values sent between devices are 32-bit elements.
A program may use at most 768 MiB of HBM per device.

v0:
```python
import jax
import jax.numpy as jnp
from jax import lax
from jax.sharding import PartitionSpec as P

LN_EPS = 1e-5
ROPE_BASE = 10000.0
NEG_FILL = -1e30


def layer_norm(hidden, ln_gamma, ln_beta):
    hidden_f32 = hidden.astype(jnp.float32)
    row_mean = jnp.mean(hidden_f32, axis=-1, keepdims=True)
    centered = hidden_f32 - row_mean
    row_var = jnp.mean(centered * centered, axis=-1, keepdims=True)
    return (centered * lax.rsqrt(row_var + LN_EPS) * ln_gamma + ln_beta).astype(jnp.bfloat16)


def rotary_tables(positions, head_dim):
    inv_freq = 1.0 / (ROPE_BASE ** (jnp.arange(0, head_dim, 2, dtype=jnp.float32) / head_dim))
    angles = positions.astype(jnp.float32)[:, None] * inv_freq[None, :]
    cos_half = jnp.cos(angles)
    sin_half = jnp.sin(angles)
    return jnp.concatenate([cos_half, cos_half], axis=-1), jnp.concatenate([sin_half, sin_half], axis=-1)


def apply_rotary(vecs, cos_full, sin_full):
    vecs_f32 = vecs.astype(jnp.float32)
    half_dim = vecs.shape[-1] // 2
    rotated = jnp.concatenate([-vecs_f32[..., half_dim:], vecs_f32[..., :half_dim]], axis=-1)
    return (vecs_f32 * cos_full + rotated * sin_full).astype(jnp.bfloat16)


def local_stats(q_rot, k_block, v_block, local_pos):
    head_dim = q_rot.shape[-1]
    slot_ids = jnp.arange(k_block.shape[1])
    scores = jnp.einsum('bhd,bsd->bhs', q_rot, k_block, preferred_element_type=jnp.float32) * head_dim ** -0.5
    valid_mask = (slot_ids[None, :] <= local_pos[:, None])[:, None, :]
    masked = jnp.where(valid_mask, scores, NEG_FILL)
    block_max = jnp.max(masked, axis=-1)
    exp_scores = jnp.where(valid_mask, jnp.exp(masked - block_max[..., None]), 0.0)
    block_sum = jnp.sum(exp_scores, axis=-1)
    block_ctx = jnp.einsum('bhs,bsd->bhd', exp_scores.astype(jnp.bfloat16), v_block, preferred_element_type=jnp.float32)
    return jnp.concatenate([block_ctx, block_max[..., None], block_sum[..., None]], axis=-1)


def combine_stats(all_stats):
    head_dim = all_stats.shape[-1] - 2
    block_max = all_stats[..., head_dim]
    top_max = jnp.max(block_max, axis=0)
    scale_w = jnp.exp(block_max - top_max[None])
    total_sum = jnp.sum(all_stats[..., head_dim + 1] * scale_w, axis=0)
    total_ctx = jnp.sum(all_stats[..., :head_dim] * scale_w[..., None], axis=0)
    return (total_ctx / total_sum[..., None]).astype(jnp.bfloat16)


def device_step(hidden, ln_gamma, ln_beta, w_qkv, w_out, w_up, w_down, k_cache, v_cache, positions):
    batch_rows = hidden.shape[0]
    seq_dev, head_dim = k_cache.shape[1], k_cache.shape[2]
    num_heads = w_out.shape[0] // head_dim
    normed = layer_norm(hidden, ln_gamma, ln_beta)
    qkv_proj = jnp.dot(normed, w_qkv, preferred_element_type=jnp.float32).astype(jnp.bfloat16)
    qkv_proj = qkv_proj.reshape(batch_rows, num_heads + 2, head_dim)
    cos_full, sin_full = rotary_tables(positions, head_dim)
    q_rot = apply_rotary(qkv_proj[:, :num_heads], cos_full[:, None, :], sin_full[:, None, :])
    k_rot = apply_rotary(qkv_proj[:, num_heads], cos_full, sin_full)
    v_new = qkv_proj[:, num_heads + 1]
    local_pos = positions - lax.axis_index('sp') * seq_dev
    write_mask = (jnp.arange(seq_dev)[None, :] == local_pos[:, None])[:, :, None]
    k_next = jnp.where(write_mask, k_rot[:, None, :], k_cache)
    v_next = jnp.where(write_mask, v_new[:, None, :], v_cache)
    block_stats = local_stats(q_rot, k_next, v_next, local_pos)
    all_stats = lax.all_gather(block_stats, 'sp')
    context = combine_stats(all_stats).reshape(batch_rows, num_heads * head_dim)
    attn_out = jnp.dot(context, w_out, preferred_element_type=jnp.float32)
    up_proj = jnp.dot(normed, w_up, preferred_element_type=jnp.float32)
    activated = jax.nn.gelu(up_proj, approximate=False).astype(jnp.bfloat16)
    mlp_part = jnp.dot(activated, w_down, preferred_element_type=jnp.float32)
    mlp_out = lax.psum(mlp_part, 'sp')
    out_hidden = (hidden.astype(jnp.float32) + attn_out + mlp_out).astype(jnp.bfloat16)
    return out_hidden, k_next, v_next


def solution(mesh):
    cache_spec = P('dp', 'sp', None)
    in_specs = (P('dp', None), P(None), P(None), P(None, None), P(None, None), P(None, 'sp'), P('sp', None), cache_spec, cache_spec, P('dp'))
    out_specs = (P('dp', None), cache_spec, cache_spec)
    return jax.shard_map(device_step, mesh=mesh, in_specs=in_specs, out_specs=out_specs, check_vma=False)
```

profile of v0, /device:TPU:113, one launch (start us, length us, event | category | flops | bytes accessed | tf_op | source)
XLA Modules:
  0.0 360.4 jit_solution(7504828608380856086)
XLA Ops:
  7.3 1.3 fusion.109
  8.6 0.8 multiply_cosine_fusion
  9.5 1.9 convert_reduce_fusion
  11.4 1.9 fusion.12
  13.3 25.8 %convolution_convert_fusion = bf16[128,4672]{0,1:T(8,128)(2,1)S(1)} fusion(bf16[4544,4672]{1,0:T(8,128)(2,1)} %param.13, bf16[128,4544]{0,1:T(8,128)(2,1)S(1)} %copy-done, f32[4544]{0:T(1024)S(1)} %copy-done.5, f32[4544]{0:T(1024)S(1)} %copy-done.7, f32[128]{0:T(128)S(1)} %add_rsqrt_fusion, f32[128]{0:T(128)S(1)} %broadcast_multiply_fusion), kind=kOutput, calls=%fused_computation.13 | convolution fusion | flops 5438857216 | bytes 44855808 | tf_op jit(solution)/shard_map/dot_general | solution.py:62
  39.2 1.0 copy-done.1
  40.2 1.1 slice.40
  41.3 3.3 copy.35
  44.6 2.5 convert_element_type.51
  47.1 1.5 slice.42
  50.2 0.8 iota_compare_fusion.1
  51.0 1.4 pad_maximum_fusion.1
  52.4 1.5 copy.26
  53.9 1.5 copy.27
  55.4 3.2 slice_negate_fusion
  58.6 23.0 %broadcast_select_fusion = (bf16[128,1024,64]{1,2,0:T(8,128)(2,1)}, bf16[128,1024,64]{1,2,0:T(8,128)(2,1)}) fusion(bf16[128,1024,64]{1,2,0:T(8,128)(2,1)} %param.18, pred[128,1024]{1,0:T(8,128)(4,1)S(1)} %get-tuple-element.16, bf16[128,64]{1,0:T(8,128)(2,1)S(1)} %copy-done.4, bf16[128,1024,64]{1,2,0:T(8,128)(2,1)} %param.17, bf16[128,64]{1,0:T(8,128)(2,1)S(1)} %copy.28), kind=kLoop, calls=%fused_computation.8 | loop fusion | flops 16777216 | bytes 67272704 | tf_op jit(solution)/shard_map/jit(_where)/select_n | solution.py:71
  81.6 22.4 %fusion = (f32[128,71]{1,0:T(8,128)S(1)}, f32[128,71,1024]{2,1,0:T(8,128)}) fusion(pred[128,1024]{1,0:T(8,128)(4,1)S(1)} %get-tuple-element.15, bf16[128,1024,64]{1,2,0:T(8,128)(2,1)} %get-tuple-element.9, f32[128,71,32]{1,2,0:T(8,128)} %slice.42, f32[128,71,32]{1,2,0:T(8,128)} %slice_negate_fusion, f32[128,64]{1,0:T(8,128)S(1)} %copy-done.3, ...), kind=kOutput, calls=%fused_computation.3 | convolution fusion | flops 1222581376 | bytes 57724416 | tf_op jit(solution)/shard_map/bhd,bsd->bhs/dot_general | solution.py:37
  103.9 18.6 %fusion.1 = f32[128,71]{1,0:T(8,128)S(1)} fusion(f32[128,71,1024]{2,1,0:T(8,128)} %get-tuple-element.20, f32[128,71]{1,0:T(8,128)S(1)} %get-tuple-element.19, pred[128,1024]{1,0:T(8,128)(4,1)S(1)} %get-tuple-element.15), kind=kLoop, calls=%fused_computation.4 | loop fusion | flops 46521472 | bytes 37428224 | tf_op jit(solution)/shard_map/reduce_sum | solution.py:42
  122.6 22.4 %fusion.3 = f32[128,71,64]{1,2,0:T(8,128)} fusion(bf16[128,1024,64]{1,2,0:T(8,128)(2,1)} %get-tuple-element.8, f32[128,71,1024]{2,1,0:T(8,128)} %get-tuple-element.20, f32[128,71]{1,0:T(8,128)S(1)} %get-tuple-element.19, pred[128,1024]{1,0:T(8,128)(4,1)S(1)} %get-tuple-element.15), kind=kOutput, calls=%fused_computation.6 | convolution fusion | flops 1237712896 | bytes 56495616 | tf_op jit(solution)/shard_map/bhs,bsd->bhd/dot_general | solution.py:43
  145.0 4.9 %pad_maximum_fusion = f32[128,71,66]{1,2,0:T(8,128)} fusion(f32[128,71,1]{1,2,0:T(1,128)S(1)} %bitcast.42, f32[128,71,1]{1,2,0:T(1,128)S(1)} %bitcast.41, f32[128,71,64]{1,2,0:T(8,128)} %fusion.3), kind=kLoop, calls=%fused_computation.14 | loop fusion | flops 1199616 | bytes 4798464 | tf_op jit(solution)/shard_map/concatenate | solution.py:44
  149.9 5.3 %copy.30 = f32[128,71,66]{0,1,2:T(8,128)} copy(f32[128,71,66]{1,2,0:T(8,128)} %pad_maximum_fusion) | data formatting | bytes 4798464 | tf_op jit(solution)/shard_map/concatenate | solution.py:44
  156.0 12.9 %fusion.105 = f32[128,2272]{0,1:T(8,128)S(1)} fusion(bf16[4544,2272]{1,0:T(8,128)(2,1)} %param.15, bf16[128,4544]{0,1:T(8,128)(2,1)S(1)} %copy-done, f32[4544]{0:T(1024)S(1)} %copy-done.6, f32[4544]{0:T(1024)S(1)} %copy-done.8, f32[128]{0:T(128)S(1)} %copy-done.12, f32[128]{0:T(128)S(1)} %copy-done.10), kind=kOutput, calls=%fused_computation.144 | convolution fusion | flops 2646425600 | bytes 23011840 | tf_op jit(solution)/shard_map/dot_general | solution.py:76
  168.9 14.8 %fusion.31 = f32[128,4544]{0,1:T(8,128)} fusion(bf16[2272,4544]{1,0:T(8,128)(2,1)} %param.16, f32[128,2272]{0,1:T(8,128)S(1)} %fusion.105), kind=kOutput, calls=%fused_computation.51 | convolution fusion | flops 2661838848 | bytes 24137728 | tf_op jit(solution)/shard_map/dot_general | solution.py:78
  183.8 72.4 %all-gather.3.cloned.1.call-done = f32[1024,71,66]{0,1,2:T(8,128)} async-done(((f32[128,71,66]{0,1,2:T(8,128)}), f32[1024,71,66]{0,1,2:T(8,128)}) %all-gather.3.cloned.1.call-update) | async-done | bytes 19193872 | tf_op jit(solution)/shard_map/all_gather | solution.py:73
  256.2 20.3 %reshape.201 = f32[8,128,71,66]{1,0,2,3:T(8,128)} reshape(f32[1024,71,66]{0,1,2:T(8,128)} %all-gather.3.cloned.1.call-done) | data formatting | bytes 38387712 | tf_op jit(solution)/shard_map/all_gather | solution.py:73
  276.5 1.1 fusion.108
  277.6 12.3 %slice.47 = f32[8,128,71,64]{1,0,2,3:T(8,128)} slice(f32[8,128,71,66]{1,0,2,3:T(8,128)} %reshape.201), slice={[0:8], [0:128], [0:71], [0:64]} | slice | bytes 37224448 | tf_op jit(solution)/shard_map/slice | solution.py:53
  290.3 20.8 %copy.36 = f32[8,128,71,64]{2,3,1,0:T(8,128)} copy(f32[8,128,71,64]{1,0,2,3:T(8,128)} %slice.47) | data formatting | bytes 37224448
  311.2 16.0 %multiply_reduce_fusion = f32[128,71,64]{1,2,0:T(8,128)} fusion(f32[8,128,71,64]{2,3,1,0:T(8,128)} %copy.36, f32[8,128,71]{2,1,0:T(8,128)S(1)} %exponential_bitcast_fusion), kind=kLoop, calls=%fused_computation.2 | loop fusion | flops 8724480 | bytes 21229568 | tf_op jit(solution)/shard_map/reduce_sum | solution.py:53
  327.5 2.9 divide_convert_fusion
  330.4 3.1 copy.34
  333.4 20.1 %fusion.7 = bf16[128,4544]{0,1:T(8,128)(2,1)} fusion(f32[128,4544]{0,1:T(8,128)} %all-reduce.2.cloned.1.call-done, bf16[128,4544]{0,1:T(8,128)(2,1)} %bitcast.37, bf16[4544,4544]{1,0:T(8,128)(2,1)} %param.14, bf16[128,4544]{0,1:T(8,128)(2,1)S(1)} %copy-done), kind=kOutput, calls=%fused_computation.12 | convolution fusion | flops 5288198144 | bytes 47112192 | tf_op jit(solution)/shard_map/dot_general | solution.py:75
  (44 shorter events, 3.4 us)
Async XLA Ops:
  7.2 6.1 %copy-start = (bf16[128,4544]{0,1:T(8,128)(2,1)S(1)}, bf16[128,4544]{0,1:T(8,128)(2,1)}, u32[]{:S(2)}) copy-start(bf16[128,4544]{0,1:T(8,128)(2,1)} %param.10) | copy-start | bytes 3489796
  7.2 6.1 %copy-start.7 = (f32[4544]{0:T(1024)S(1)}, f32[4544]{0:T(1024)}, u32[]{:S(2)}) copy-start(f32[4544]{0:T(1024)} %param.11) | copy-start | bytes 54532
  7.2 6.1 %copy-start.5 = (f32[4544]{0:T(1024)S(1)}, f32[4544]{0:T(1024)}, u32[]{:S(2)}) copy-start(f32[4544]{0:T(1024)} %param.12) | copy-start | bytes 54532
  7.2 248.9 %all-gather.3.cloned.1.call-start = ((), (), s32[]{:S(2)}) async-start(), calls=%async_computation.1 | async-start | bytes 21897216 | tf_op jit(solution)/shard_map/all_gather | solution.py:73
  11.4 27.8 %copy-start.9 = (f32[128]{0:T(128)}, f32[128]{0:T(128)S(1)}, u32[]{:S(2)}) copy-start(f32[128]{0:T(128)S(1)} %broadcast_multiply_fusion) | copy-start | bytes 1540
  13.3 25.9 %copy-start.11 = (f32[128]{0:T(128)}, f32[128]{0:T(128)S(1)}, u32[]{:S(2)}) copy-start(f32[128]{0:T(128)S(1)} %add_rsqrt_fusion) | copy-start | bytes 1540
  39.2 1.0 copy-start.1
  55.4 3.2 copy-start.4
  58.6 23.0 %copy-start.2 = (f32[128,64]{1,0:T(8,128)S(1)}, f32[128,64]{1,0:T(8,128)}, u32[]{:S(2)}) copy-start(f32[128,64]{1,0:T(8,128)} %copy.26) | copy-start | bytes 98308
  58.6 23.0 %copy-start.3 = (f32[128,64]{1,0:T(8,128)S(1)}, f32[128,64]{1,0:T(8,128)}, u32[]{:S(2)}) copy-start(f32[128,64]{1,0:T(8,128)} %copy.27) | copy-start | bytes 98308
  155.3 0.7 copy-start.6
  155.3 0.7 copy-start.8
  155.3 0.7 copy-start.10
  155.3 0.7 copy-start.12
  155.3 178.1 %all-reduce.2.cloned.1.call-start = ((), (), s32[]{:S(2)}) async-start(), calls=%async_computation | async-start | bytes 4653056 | tf_op jit(solution)/shard_map/psum | solution.py:79
Sparse Core Ops, SparseCore 0:
  155.5 100.6 all-gather.2
  258.6 56.6 all-reduce.1
where the time goes:
time: 362 us; the launch traced here: 360 us
  matrix products  118 us (33%)
  other arithmetic  81.3 us (22%)
  local copies, waits for them, and re-layouts  73.8 us (20%)
  waiting for transfers between devices  72.5 us (20%)
  between operations  14.3 us (4%)
    all_gather x1, waiting for transfers between devices, device_step(): all_stats = lax.all_gather(block_stats, 'sp')  72.4 us
    unnamed x31, local copies, waits for them, and re-layouts  26.4 us
    dot_general x1, matrix products, device_step(): jnp.dot(normed, w_qkv, preferred_element_type=jnp.float32)  25.8 us
    select_n x1, other arithmetic, device_step(): v_next = jnp.where(write_mask, v_new[:, None, :], v_cache)  23 us
    dot_general x1, matrix products, local_stats(): jnp.einsum('bhs,bsd->bhd', exp_scores.astype(jnp.bfloat16), v_block, pref...  22.4 us
    dot_general x1, matrix products, local_stats(): jnp.einsum('bhd,bsd->bhs', q_rot, k_block, preferred_element_type=jnp.flo...  22.4 us
    all_gather x1, local copies, waits for them, and re-layouts, device_step(): all_stats = lax.all_gather(block_stats, 'sp')  20.3 us
    dot_general x1, matrix products, device_step(): attn_out = jnp.dot(context, w_out, preferred_element_type=jnp.float32)  20.1 us
  transfers between devices with their start and end apart: 2, of which 1 were waited for; matrix products, arithmetic and copies ran while one was open for 29% of the time, Pallas kernels for 0%

commit v1 on v0

v1 whole, which is shorter than its diff:
```python
import functools

import jax
import jax.numpy as jnp
from jax import lax
from jax.experimental import pallas as pl
from jax.experimental.pallas import tpu as pltpu
from jax.sharding import PartitionSpec as P

LN_EPS = 1e-5
ROPE_BASE = 10000.0
NEG_FILL = -1e30
LANES = 128
ROWS_PER_CHUNK = 4
SLOTS = 6
AHEAD = 4


def layer_norm(hidden, ln_gamma, ln_beta):
    hidden_f32 = hidden.astype(jnp.float32)
    row_mean = jnp.mean(hidden_f32, axis=-1, keepdims=True)
    centered = hidden_f32 - row_mean
    row_var = jnp.mean(centered * centered, axis=-1, keepdims=True)
    return (centered * lax.rsqrt(row_var + LN_EPS) * ln_gamma + ln_beta).astype(jnp.bfloat16)


def rotary_tables(positions, head_dim):
    inv_freq = 1.0 / (ROPE_BASE ** (jnp.arange(0, head_dim, 2, dtype=jnp.float32) / head_dim))
    angles = positions.astype(jnp.float32)[:, None] * inv_freq[None, :]
    cos_half = jnp.cos(angles)
    sin_half = jnp.sin(angles)
    reps = 2 * LANES // head_dim
    return jnp.concatenate([cos_half] * reps, axis=-1), jnp.concatenate([sin_half] * reps, axis=-1)


def attention_kernel(num_pairs, pos_ref, qkv_ref, cos_ref, sin_ref, k_in, v_in, k_out, v_out, stats_ref,
                     q_s, k_new, v_new, k_buf, v_buf, in_sem, out_sem):
    rows, dim = qkv_ref.shape[0], k_in.shape[1]
    seq = k_in.shape[2]
    heads = 2 * num_pairs
    chunks = rows // ROWS_PER_CHUNK
    own_rows = rows // stats_ref.shape[0]

    def copies(chunk, slot):
        window = pl.ds(chunk * ROWS_PER_CHUNK, ROWS_PER_CHUNK)
        return (pltpu.make_async_copy(k_in.at[window], k_buf.at[slot], in_sem.at[0, slot]),
                pltpu.make_async_copy(v_in.at[window], v_buf.at[slot], in_sem.at[1, slot]))

    def stores(chunk, slot):
        window = pl.ds(chunk * ROWS_PER_CHUNK, ROWS_PER_CHUNK)
        return (pltpu.make_async_copy(k_buf.at[slot], k_out.at[window], out_sem.at[0, slot]),
                pltpu.make_async_copy(v_buf.at[slot], v_out.at[window], out_sem.at[1, slot]))

    for chunk in range(AHEAD):
        for copy in copies(chunk, chunk):
            copy.start()

    lane = lax.broadcasted_iota(jnp.int32, (rows, LANES), 1)
    row = lax.broadcasted_iota(jnp.int32, (rows, LANES), 0)
    low = lane < dim
    first_half = lax.rem(lane, dim) < dim // 2
    mine = (lax.rem(row, 2) == 0) == low

    def rope(x):
        rot = jnp.where(first_half, -pltpu.roll(x, LANES - dim // 2, 1), pltpu.roll(x, dim // 2, 1))
        y = x * cos_ref[...] + rot * sin_ref[...]
        return y.astype(jnp.bfloat16).astype(jnp.float32)

    def prepare(pair, carry):
        x = qkv_ref[:, pl.ds(pl.multiple_of(pair * LANES, LANES), LANES)].astype(jnp.float32)
        y = rope(x) * dim ** -0.5
        swapped = pltpu.roll(y, dim, 1)
        base = pl.multiple_of(pair * 2 * rows, 2 * rows)
        q_s[pl.ds(base, rows), :] = jnp.where(mine, jnp.where(low, y, swapped), 0.0)
        q_s[pl.ds(base + rows, rows), :] = jnp.where(mine, jnp.where(low, swapped, y), 0.0)
        return carry

    lax.fori_loop(0, num_pairs, prepare, 0)
    last = (num_pairs - 1) * LANES
    k_new[...] = rope(qkv_ref[:, last:last + LANES].astype(jnp.float32)).T[dim:, :]
    v_new[...] = qkv_ref[:, last + LANES:last + LANES + dim].astype(jnp.float32).T

    dim_lane = lax.broadcasted_iota(jnp.int32, (dim, LANES), 1)
    slot_ids = lax.broadcasted_iota(jnp.int32, (1, seq), 1)
    head_lane = lax.broadcasted_iota(jnp.int32, (heads, LANES), 1)

    def step(chunk, carry):
        slot = lax.rem(chunk, SLOTS)
        for copy in copies(chunk, slot):
            copy.wait()
        for r in range(ROWS_PER_CHUNK):
            b = chunk * ROWS_PER_CHUNK + r
            at = pos_ref[b]

            @pl.when((at >= 0) & (at < seq))
            def _():
                start = pl.multiple_of((at // LANES) * LANES, LANES)
                hit = dim_lane == at - start
                for new, buf in ((k_new, k_buf), (v_new, v_buf)):
                    column = jnp.sum(jnp.where(dim_lane == b, new[...], 0.0), axis=1, keepdims=True)
                    old = buf[slot, r, :, pl.ds(start, LANES)].astype(jnp.float32)
                    buf[slot, r, :, pl.ds(start, LANES)] = jnp.where(hit, column, old).astype(jnp.bfloat16)

        for copy in stores(chunk, slot):
            copy.start()

        @pl.when(chunk + AHEAD < chunks)
        def _():
            ahead = lax.rem(chunk + AHEAD, SLOTS)

            @pl.when(chunk + AHEAD >= SLOTS)
            def _():
                for copy in stores(chunk + AHEAD - SLOTS, ahead):
                    copy.wait()

            for copy in copies(chunk + AHEAD, ahead):
                copy.start()

        owner = (chunk * ROWS_PER_CHUNK) // own_rows
        for half in range(ROWS_PER_CHUNK // 2):
            keys = k_buf[slot, 2 * half:2 * half + 2].reshape(2 * dim, seq)
            values = v_buf[slot, 2 * half:2 * half + 2].reshape(2 * dim, seq)
            parts = []
            for r in (2 * half, 2 * half + 1):
                b = chunk * ROWS_PER_CHUNK + r
                at = pos_ref[b]
                q = q_s[pl.ds(b, heads, stride=rows), :].astype(jnp.bfloat16)
                s = jnp.dot(q, keys, preferred_element_type=jnp.float32)
                s = jnp.where(slot_ids <= at, s, NEG_FILL)
                m = jnp.max(s, axis=1, keepdims=True)
                e = jnp.exp(s - jnp.where(at >= 0, m, 0.0))
                total = jnp.sum(e, axis=1, keepdims=True)
                o = lax.dot_general(e.astype(jnp.bfloat16), values, (((1,), (1,)), ((), ())),
                                    preferred_element_type=jnp.float32)
                parts.append(o)
                local = lax.rem(b, own_rows)
                table = stats_ref[owner, own_rows // 2]
                table = jnp.where(head_lane == local, m, jnp.where(head_lane == own_rows + local, total, table))
                stats_ref[owner, own_rows // 2] = table
            pair = lax.rem(chunk * ROWS_PER_CHUNK, own_rows) // 2 + half
            stats_ref[owner, pair] = jnp.where(head_lane < dim, parts[0], parts[1])
        return carry

    lax.fori_loop(0, chunks, step, 0)
    for chunk in range(chunks - SLOTS, chunks):
        for copy in stores(chunk, chunk % SLOTS):
            copy.wait()


def attention(local_pos, qkv, cos_full, sin_full, k_t, v_t, owners):
    rows, dim, seq = k_t.shape
    num_pairs = (qkv.shape[1] // dim - 1) // 2
    own_rows = rows // owners
    vmem = pl.BlockSpec(memory_space=pltpu.VMEM)
    hbm = pl.BlockSpec(memory_space=pl.ANY)
    return pl.pallas_call(
        functools.partial(attention_kernel, num_pairs),
        out_shape=(jax.ShapeDtypeStruct(k_t.shape, k_t.dtype), jax.ShapeDtypeStruct(v_t.shape, v_t.dtype),
                   jax.ShapeDtypeStruct((owners, own_rows // 2 + 1, 2 * num_pairs, LANES), jnp.float32)),
        in_specs=[pl.BlockSpec(memory_space=pltpu.SMEM), vmem, vmem, vmem, hbm, hbm],
        out_specs=(hbm, hbm, vmem),
        scratch_shapes=[
            pltpu.VMEM((2 * num_pairs * rows, LANES), jnp.float32),
            pltpu.VMEM((dim, LANES), jnp.float32),
            pltpu.VMEM((dim, LANES), jnp.float32),
            pltpu.VMEM((SLOTS, ROWS_PER_CHUNK, dim, seq), k_t.dtype),
            pltpu.VMEM((SLOTS, ROWS_PER_CHUNK, dim, seq), v_t.dtype),
            pltpu.SemaphoreType.DMA((2, SLOTS)),
            pltpu.SemaphoreType.DMA((2, SLOTS)),
        ],
        compiler_params=pltpu.CompilerParams(vmem_limit_bytes=48 * 2 ** 20),
        cost_estimate=pl.CostEstimate(flops=4 * rows * 2 * num_pairs * seq * dim, transcendentals=0,
                                      bytes_accessed=8 * rows * dim * seq),
    )(local_pos, qkv, cos_full, sin_full, k_t, v_t)


def combine(gathered, dim, heads):
    own_rows = (gathered.shape[1] - 1) * 2
    block_max = gathered[:, -1, :, :own_rows]
    block_sum = gathered[:, -1, :, own_rows:2 * own_rows]
    scale_w = jnp.exp(block_max - jnp.max(block_max, axis=0)[None])
    total_sum = jnp.sum(block_sum * scale_w, axis=0)
    sources, pairs, slots, _ = gathered[:, :-1].shape
    parts = gathered[:, :-1].reshape(sources, pairs, slots, 2, dim)
    weights = scale_w.reshape(sources, slots, pairs, 2).transpose(0, 2, 1, 3)
    total_ctx = jnp.sum(parts * weights[..., None], axis=0)
    ctx = total_ctx / total_sum.reshape(slots, pairs, 2).transpose(1, 0, 2)[..., None]
    ctx = ctx[:, :heads].transpose(0, 2, 1, 3).reshape(own_rows, heads * dim)
    return ctx.astype(jnp.bfloat16)


def device_step(hidden, ln_gamma, ln_beta, w_qkv, w_out, w_up, w_down, k_cache, v_cache, positions):
    seq_dev, head_dim = k_cache.shape[1], k_cache.shape[2]
    num_heads = w_out.shape[0] // head_dim
    group = lax.axis_size('sp')
    me = lax.axis_index('sp')
    normed = layer_norm(hidden, ln_gamma, ln_beta)
    qkv = jnp.dot(normed, w_qkv, preferred_element_type=jnp.float32).astype(jnp.bfloat16)
    cos_full, sin_full = rotary_tables(positions, head_dim)
    local_pos = positions - me * seq_dev
    k_t, v_t = jnp.swapaxes(k_cache, 1, 2), jnp.swapaxes(v_cache, 1, 2)
    k_next, v_next, stats = attention(local_pos, qkv, cos_full, sin_full, k_t, v_t, group)
    gathered = lax.all_to_all(stats, 'sp', 0, 0, tiled=True)
    context = combine(gathered, head_dim, num_heads)
    attn_out = jnp.dot(context, w_out, preferred_element_type=jnp.float32)
    up_proj = jnp.dot(normed, w_up, preferred_element_type=jnp.float32)
    activated = jax.nn.gelu(up_proj, approximate=False).astype(jnp.bfloat16)
    mlp_part = jnp.dot(activated, w_down, preferred_element_type=jnp.float32)
    mlp_own = lax.psum_scatter(mlp_part, 'sp', scatter_dimension=0, tiled=True)
    out_all = lax.all_gather(attn_out + mlp_own, 'sp', axis=0, tiled=True)
    out_hidden = (hidden.astype(jnp.float32) + out_all).astype(jnp.bfloat16)
    return out_hidden, jnp.swapaxes(k_next, 1, 2), jnp.swapaxes(v_next, 1, 2)


def solution(mesh):
    cache_spec = P('dp', 'sp', None)
    in_specs = (P('dp', None), P(None), P(None), P(None, None), P(None, None), P(None, 'sp'), P('sp', None), cache_spec, cache_spec, P('dp'))
    out_specs = (P('dp', None), cache_spec, cache_spec)
    return jax.shard_map(device_step, mesh=mesh, in_specs=in_specs, out_specs=out_specs, check_vma=False)
```

time: 362 us -> 226 us (0.62)
  other arithmetic: 81.3 us -> 8.39 us
  matrix products: 118 us -> 65.1 us
  Pallas kernels: 0 us -> 51.4 us
  local copies, waits for them, and re-layouts: 73.8 us -> 22.5 us
  waiting for transfers between devices: 72.5 us -> 22.6 us
  blocking collectives: 0 us -> 41.4 us
    pallas_call x0 -> x1, Pallas kernels: none -> 51.4 us  [attention(): pl.pallas_call(functools.partial(attention_kernel, num_pairs), out_shape=...]
    all_gather x1, waiting for transfers between devices: 72.4 us -> 22.5 us  [device_step(): out_all = lax.all_gather(attn_out + mlp_own, 'sp', axis=0, tiled=True)]
    dot_general x2 -> x0, matrix products: 44.8 us -> none  [the longest x1 22.4 us: local_stats(): jnp.einsum('bhs,bsd->bhd', exp_scores.astype(jnp.bfloat16), v_block, pref...]
    all_to_all x0 -> x1, blocking collectives: none -> 41.4 us  [device_step(): gathered = lax.all_to_all(stats, 'sp', 0, 0, tiled=True)]
    reduce_sum x3 -> x2, other arithmetic: 34.7 us -> 3.84 us  [the longest x1 2.63 us: combine(): total_ctx = jnp.sum(parts * weights[..., None], axis=0)]
    select_n x1 -> x0, other arithmetic: 23 us -> none  [device_step(): v_next = jnp.where(write_mask, v_new[:, None, :], v_cache)]
    all_gather x1 -> x0, local copies, waits for them, and re-layouts: 20.3 us -> none  [device_step(): all_stats = lax.all_gather(block_stats, 'sp')]
    unnamed x31 -> x14, local copies, waits for them, and re-layouts: 26.4 us -> 6.33 us
  transfers between devices with their start and end apart: 2 -> 2, of which waited for: 1 -> 1; matrix products, arithmetic and copies ran while one was open for 29% -> 20% of each run, Pallas kernels for 0% -> 23%
where the time goes in v1:
time: 226 us
  matrix products  65.1 us (29%)
  Pallas kernels  51.4 us (23%)
  blocking collectives  41.4 us (18%)
  waiting for transfers between devices  22.6 us (10%)
  local copies, waits for them, and re-layouts  22.5 us (10%)
  between operations  14.3 us (6%)
  other arithmetic  8.39 us (4%)
    pallas_call x1, Pallas kernels, attention(): pl.pallas_call(functools.partial(attention_kernel, num_pairs), out_shape=...  51.4 us
    all_to_all x1, blocking collectives, device_step(): gathered = lax.all_to_all(stats, 'sp', 0, 0, tiled=True)  41.4 us
    all_gather x1, waiting for transfers between devices, device_step(): out_all = lax.all_gather(attn_out + mlp_own, 'sp', axis=0, tiled=True)  22.5 us
    dot_general x1, matrix products, device_step(): jnp.dot(normed, w_qkv, preferred_element_type=jnp.float32)  22.3 us
    dot_general x1, matrix products, device_step(): attn_out = jnp.dot(context, w_out, preferred_element_type=jnp.float32)  16.6 us
    dot_general x1, matrix products, device_step(): mlp_part = jnp.dot(activated, w_down, preferred_element_type=jnp.float32)  13.6 us
    dot_general x1, matrix products, device_step(): up_proj = jnp.dot(normed, w_up, preferred_element_type=jnp.float32)  12.7 us
    mul x2, local copies, waits for them, and re-layouts, combine(): total_ctx = jnp.sum(parts * weights[..., None], axis=0)  11 us
  transfers between devices with their start and end apart: 2, of which 1 were waited for; matrix products, arithmetic and copies ran while one was open for 20% of the time, Pallas kernels for 23%

profile of v1, /device:TPU:113, one launch (start us, length us, event | category | flops | bytes accessed | tf_op | source)
XLA Modules:
  0.0 226.0 jit_solution(561502164121507906)
XLA Ops:
  7.2 0.1 reduce-scatter.2.cloned.1.call-start
  7.2 1.6 copy.37
  8.9 0.3 convert_reduce_fusion
  9.1 0.5 fusion.2
  9.6 12.7 %fusion.86 = f32[128,2272]{0,1:T(8,128)S(1)} fusion(bf16[4544,2272]{1,0:T(8,128)(2,1)} %param.15, bf16[128,4544]{1,0:T(8,128)(2,1)S(1)} %copy.37, f32[4544]{0:T(1024)S(1)} %copy-done.2, f32[4544]{0:T(1024)S(1)} %copy-done.3, f32[128]{0:T(128)S(1)} %add_rsqrt_fusion, f32[128]{0:T(128)S(1)} %broadcast_multiply_fusion), kind=kOutput, calls=%fused_computation.113 | convolution fusion | flops 2646425600 | bytes 23011840 | tf_op jit(solution)/shard_map/dot_general | solution.py:206
  22.3 13.6 %fusion.18 = f32[128,4544]{1,0:T(8,128)} fusion(bf16[2272,4544]{1,0:T(8,128)(2,1)} %param.16, f32[128,2272]{0,1:T(8,128)S(1)} %fusion.86), kind=kOutput, calls=%fused_computation.33 | convolution fusion | flops 2661838848 | bytes 24137728 | tf_op jit(solution)/shard_map/dot_general | solution.py:208
  35.9 0.2 all-gather.2.cloned.1.call-start
  36.2 22.3 %convolution_convert_fusion = bf16[128,4672]{0,1:T(8,128)(2,1)} fusion(bf16[4544,4672]{1,0:T(8,128)(2,1)} %param.13, bf16[128,4544]{1,0:T(8,128)(2,1)S(1)} %copy.37, f32[4544]{0:T(1024)S(1)} %copy-done.2, f32[4544]{0:T(1024)S(1)} %copy-done.3, f32[128]{0:T(128)S(1)} %add_rsqrt_fusion, f32[128]{0:T(128)S(1)} %broadcast_multiply_fusion), kind=kOutput, calls=%fused_computation | convolution fusion | flops 5438857216 | bytes 44855808 | tf_op jit(solution)/shard_map/dot_general | solution.py:198
  58.4 1.7 copy.38.qkv_ref
  60.2 0.3 multiply_sine_fusion
  60.5 0.2 pad_maximum_fusion
  60.7 51.4 %shard_map.121 = (bf16[128,64,1024]{2,1,0:T(8,128)(2,1)}, bf16[128,64,1024]{2,1,0:T(8,128)(2,1)}, f32[8,9,72,128]{3,2,1,0:T(8,128)S(1)}) custom-call(s32[128]{0:T(128)S(1)} %get-tuple-element.24.pos_ref, bf16[128,4672]{1,0:T(8,128)(2,1)S(1)} %copy.38.qkv_ref, f32[128,128]{1,0:T(8,128)S(1)} %get-tuple-element.25.cos_ref, ...), custom_call_target="tpu_custom_call" | custom-call | flops 2415919104 | bytes 67108864 | tf_op jit(solution)/shard_map/pallas_call | solution.py:156
  112.1 41.4 %all_to_all.5 = f32[8,9,72,128]{3,2,1,0:T(8,128)S(1)} all-to-all(f32[8,9,72,128]{3,2,1,0:T(8,128)S(1)} %get-tuple-element.6), channel_id=1, replica_groups=mesh['dp'=2,'sp'=8] {'sp'}, dimensions={0} | all-to-all | bytes 5308416 | tf_op jit(solution)/shard_map/all_to_all | solution.py:203
  153.5 1.5 copy-done
  155.1 0.6 copy-done.1
  155.8 1.0 slice_bitcast_fusion.1
  156.7 0.1 copy.40
  156.9 0.7 exponential_bitcast_fusion
  157.5 1.6 copy.42
  159.1 6.4 %mul.76 = f32[8,8,72,2,64]{4,3,2,1,0:T(2,128)} broadcast(f32[8,8,72,2]{3,2,1,0:T(8,128)S(1)} %copy.42), dimensions={0,1,2,3} | broadcast | bytes 2396160 | tf_op jit(solution)/shard_map/mul | solution.py:186
  165.5 4.6 %mul.77 = f32[8,8,72,128]{3,2,1,0:T(8,128)S(1)} reshape(f32[8,8,72,2,64]{4,3,2,1,0:T(2,128)} %mul.76) | data formatting | bytes 4718592 | tf_op jit(solution)/shard_map/mul | solution.py:186
  170.2 2.6 %fusion.7 = f32[8,72,128]{2,1,0:T(8,128)} fusion(f32[8,8,72,128]{3,2,1,0:T(8,128)S(1)} %mul.77, f32[8,9,72,128]{3,2,1,0:T(8,128)} %copy-done), kind=kLoop, calls=%fused_computation.13 | loop fusion | flops 1105920 | bytes 5013504 | tf_op jit(solution)/shard_map/reduce_sum | solution.py:186
  172.8 1.3 reduce_sum.41
  174.1 1.2 fusion.52
  175.3 0.1 copy.43
  175.4 0.2 copy.48
  175.6 0.8 fusion.54
  176.4 0.2 convert_element_type.31
  176.7 16.6 %convolution_add_fusion = f32[16,4544]{1,0:T(8,128)} fusion(f32[16,4544]{1,0:T(8,128)} %reduce-scatter.2.cloned.1.call-done, bf16[16,4544]{1,0:T(8,128)(2,1)S(1)} %convert_element_type.31, bf16[4544,4544]{1,0:T(8,128)(2,1)} %param.14), kind=kOutput, calls=%fused_computation.1 | convolution fusion | flops 660806656 | bytes 42022912 | tf_op jit(solution)/shard_map/dot_general | solution.py:205
  193.4 22.5 %all-gather.2.cloned.1.call-done = f32[128,4544]{1,0:T(8,128)} async-done(((f32[16,4544]{1,0:T(8,128)}), f32[128,4544]{1,0:T(8,128)}) %all-gather.2.cloned.1.call-update) | async-done | bytes 2326544 | tf_op jit(solution)/shard_map/all_gather | solution.py:210
  215.8 1.9 fusion.6
  217.7 1.4 copy.46
  (18 shorter events, 0.3 us)
Async XLA Ops:
  7.2 169.5 %reduce-scatter.2.cloned.1.call-start = ((), (), s32[]{:S(2)}) async-start(), calls=%async_computation.2 | async-start | bytes 2654208 | tf_op jit(solution)/shard_map/reduce_scatter | solution.py:209
  8.8 0.8 copy-start.2
  8.8 0.8 copy-start.3
  35.9 179.9 %all-gather.2.cloned.1.call-start = ((), (), s32[]{:S(2)}) async-start(), calls=%async_computation.3 | async-start | bytes 2654208 | tf_op jit(solution)/shard_map/all_gather | solution.py:210
  58.4 1.8 copy-start.4
  153.5 1.5 copy-start
  155.1 0.6 copy-start.1
Sparse Core Ops, SparseCore 0:
  36.0 30.1 reduce-scatter.1
  193.5 22.2 all-gather.1

commit v2 on v1

--- a/solution.py
+++ b/solution.py
@@ -11,9 +11,10 @@
 ROPE_BASE = 10000.0
 NEG_FILL = -1e30
 LANES = 128
-ROWS_PER_CHUNK = 4
+ROWS_PER_CHUNK = 8
 SLOTS = 6
 AHEAD = 4
+PAD_ROWS = 8
 
 
 def layer_norm(hidden, ln_gamma, ln_beta):
@@ -34,12 +35,16 @@
 
 
 def attention_kernel(num_pairs, pos_ref, qkv_ref, cos_ref, sin_ref, k_in, v_in, k_out, v_out, stats_ref,
-                     q_s, k_new, v_new, k_buf, v_buf, in_sem, out_sem):
+                     x_s, k_new, v_new, s_even, s_odd, e_even, e_odd, k_buf, v_buf, in_sem, out_sem):
     rows, dim = qkv_ref.shape[0], k_in.shape[1]
     seq = k_in.shape[2]
     heads = 2 * num_pairs
+    stride = rows + PAD_ROWS
     chunks = rows // ROWS_PER_CHUNK
     own_rows = rows // stats_ref.shape[0]
+    steps = ROWS_PER_CHUNK // 2
+    full = num_pairs // 8 * 8
+    tail = num_pairs - full
 
     def copies(chunk, slot):
         window = pl.ds(chunk * ROWS_PER_CHUNK, ROWS_PER_CHUNK)
@@ -55,37 +60,70 @@
         for copy in copies(chunk, chunk):
             copy.start()
 
-    lane = lax.broadcasted_iota(jnp.int32, (rows, LANES), 1)
-    row = lax.broadcasted_iota(jnp.int32, (rows, LANES), 0)
-    low = lane < dim
-    first_half = lax.rem(lane, dim) < dim // 2
-    mine = (lax.rem(row, 2) == 0) == low
-
-    def rope(x):
+    def rope(x, cos_full, sin_full):
+        lane = lax.broadcasted_iota(jnp.int32, x.shape, 1)
+        first_half = lax.rem(lane, dim) < dim // 2
         rot = jnp.where(first_half, -pltpu.roll(x, LANES - dim // 2, 1), pltpu.roll(x, dim // 2, 1))
-        y = x * cos_ref[...] + rot * sin_ref[...]
-        return y.astype(jnp.bfloat16).astype(jnp.float32)
-
-    def prepare(pair, carry):
-        x = qkv_ref[:, pl.ds(pl.multiple_of(pair * LANES, LANES), LANES)].astype(jnp.float32)
-        y = rope(x) * dim ** -0.5
-        swapped = pltpu.roll(y, dim, 1)
-        base = pl.multiple_of(pair * 2 * rows, 2 * rows)
-        q_s[pl.ds(base, rows), :] = jnp.where(mine, jnp.where(low, y, swapped), 0.0)
-        q_s[pl.ds(base + rows, rows), :] = jnp.where(mine, jnp.where(low, swapped, y), 0.0)
-        return carry
-
-    lax.fori_loop(0, num_pairs, prepare, 0)
+        return (x * cos_full + rot * sin_full).astype(jnp.bfloat16).astype(jnp.float32)
+
+    for pair in range(num_pairs):
+        x_s[pair * stride:pair * stride + rows, :] = qkv_ref[:, pair * LANES:(pair + 1) * LANES].astype(jnp.float32)
     last = (num_pairs - 1) * LANES
-    k_new[...] = rope(qkv_ref[:, last:last + LANES].astype(jnp.float32)).T[dim:, :]
+    k_new[...] = rope(qkv_ref[:, last:last + LANES].astype(jnp.float32), cos_ref[...], sin_ref[...]).T[dim:, :]
     v_new[...] = qkv_ref[:, last + LANES:last + LANES + dim].astype(jnp.float32).T
 
     dim_lane = lax.broadcasted_iota(jnp.int32, (dim, LANES), 1)
     slot_ids = lax.broadcasted_iota(jnp.int32, (1, seq), 1)
     head_lane = lax.broadcasted_iota(jnp.int32, (heads, LANES), 1)
-
-    def step(chunk, carry):
+    tail_row = lax.broadcasted_iota(jnp.int32, (8, LANES), 0)
+    scores = (s_even, s_odd)
+    weights = (e_even, e_odd)
+
+    def queries(b, low):
+        x = x_s[pl.ds(b, full + 8, stride=stride), :]
+        y = rope(x, cos_ref[pl.ds(b, 1), :], sin_ref[pl.ds(b, 1), :]) * dim ** -0.5
+        z = pltpu.roll(y, dim, 1)
+        first, second = (y, z) if low else (z, y)
+        mixed = jnp.where(tail_row < tail, first[full:], pltpu.roll(second[full:], tail, 0))
+        q = jnp.concatenate([first[:full], second[:full], mixed], axis=0)
+        keep = (head_lane < dim) == low
+        return jnp.where(keep, q, 0.0).astype(jnp.bfloat16)
+
+    def score(chunk, slot, step):
+        b = chunk * ROWS_PER_CHUNK + 2 * step
+        keys = k_buf[slot, 2 * step:2 * step + 2].reshape(2 * dim, seq)
+        q = jnp.concatenate([queries(b, True), queries(b + 1, False)], axis=0)
+        s = jnp.dot(q, keys, preferred_element_type=jnp.float32)
+        out = scores[step % 2]
+        for r in range(2):
+            out[r * heads:(r + 1) * heads, :] = jnp.where(slot_ids <= pos_ref[b + r], s[r * heads:(r + 1) * heads], NEG_FILL)
+
+    def weigh(chunk, step):
+        src, out = scores[step % 2], weights[step % 2]
+        b = chunk * ROWS_PER_CHUNK + 2 * step
+        owner = b // own_rows
+        local = lax.rem(b, own_rows)
+        table = stats_ref[owner, own_rows // 2]
+        for r in range(2):
+            s = src[r * heads:(r + 1) * heads, :]
+            m = jnp.max(s, axis=1, keepdims=True)
+            e = jnp.exp(s - jnp.where(pos_ref[b + r] >= 0, m, 0.0))
+            total = jnp.sum(e, axis=1, keepdims=True)
+            out[r * heads:(r + 1) * heads, :] = e.astype(jnp.bfloat16)
+            table = jnp.where(head_lane == local + r, m,
+                              jnp.where(head_lane == own_rows + local + r, total, table))
+        stats_ref[owner, own_rows // 2] = table
+
+    def apply(chunk, slot, step):
+        b = chunk * ROWS_PER_CHUNK + 2 * step
+        values = v_buf[slot, 2 * step:2 * step + 2].reshape(2 * dim, seq)
+        o = lax.dot_general(weights[step % 2][...], values, (((1,), (1,)), ((), ())), preferred_element_type=jnp.float32)
+        stats_ref[b // own_rows, lax.rem(b, own_rows) // 2] = jnp.where(head_lane < dim, o[:heads], o[heads:])
+
+    def body(chunk, carry):
         slot = lax.rem(chunk, SLOTS)
+        before = lax.rem(chunk + SLOTS - 1, SLOTS)
+        earlier = jnp.maximum(chunk - 1, 0)
         for copy in copies(chunk, slot):
             copy.wait()
         for r in range(ROWS_PER_CHUNK):
@@ -116,32 +154,22 @@
             for copy in copies(chunk + AHEAD, ahead):
                 copy.start()
 
-        owner = (chunk * ROWS_PER_CHUNK) // own_rows
-        for half in range(ROWS_PER_CHUNK // 2):
-            keys = k_buf[slot, 2 * half:2 * half + 2].reshape(2 * dim, seq)
-            values = v_buf[slot, 2 * half:2 * half + 2].reshape(2 * dim, seq)
-            parts = []
-            for r in (2 * half, 2 * half + 1):
-                b = chunk * ROWS_PER_CHUNK + r
-                at = pos_ref[b]
-                q = q_s[pl.ds(b, heads, stride=rows), :].astype(jnp.bfloat16)
-                s = jnp.dot(q, keys, preferred_element_type=jnp.float32)
-                s = jnp.where(slot_ids <= at, s, NEG_FILL)
-                m = jnp.max(s, axis=1, keepdims=True)
-                e = jnp.exp(s - jnp.where(at >= 0, m, 0.0))
-                total = jnp.sum(e, axis=1, keepdims=True)
-                o = lax.dot_general(e.astype(jnp.bfloat16), values, (((1,), (1,)), ((), ())),
-                                    preferred_element_type=jnp.float32)
-                parts.append(o)
-                local = lax.rem(b, own_rows)
-                table = stats_ref[owner, own_rows // 2]
-                table = jnp.where(head_lane == local, m, jnp.where(head_lane == own_rows + local, total, table))
-                stats_ref[owner, own_rows // 2] = table
-            pair = lax.rem(chunk * ROWS_PER_CHUNK, own_rows) // 2 + half
-            stats_ref[owner, pair] = jnp.where(head_lane < dim, parts[0], parts[1])
+        for step in range(steps):
+            if step >= 2:
+                apply(chunk, slot, step - 2)
+            else:
+                apply(earlier, before, step - 2 + steps)
+            score(chunk, slot, step)
+            if step >= 1:
+                weigh(chunk, step - 1)
+            else:
+                weigh(earlier, steps - 1)
         return carry
 
-    lax.fori_loop(0, chunks, step, 0)
+    lax.fori_loop(0, chunks, body, 0)
+    apply(chunks - 1, (chunks - 1) % SLOTS, steps - 2)
+    weigh(chunks - 1, steps - 1)
+    apply(chunks - 1, (chunks - 1) % SLOTS, steps - 1)
     for chunk in range(chunks - SLOTS, chunks):
         for copy in stores(chunk, chunk % SLOTS):
             copy.wait()
@@ -160,9 +188,13 @@
         in_specs=[pl.BlockSpec(memory_space=pltpu.SMEM), vmem, vmem, vmem, hbm, hbm],
         out_specs=(hbm, hbm, vmem),
         scratch_shapes=[
-            pltpu.VMEM((2 * num_pairs * rows, LANES), jnp.float32),
+            pltpu.VMEM(((num_pairs // 8 * 8 + 8) * (rows + PAD_ROWS), LANES), jnp.float32),
             pltpu.VMEM((dim, LANES), jnp.float32),
             pltpu.VMEM((dim, LANES), jnp.float32),
+            pltpu.VMEM((4 * num_pairs, seq), jnp.float32),
+            pltpu.VMEM((4 * num_pairs, seq), jnp.float32),
+            pltpu.VMEM((4 * num_pairs, seq), jnp.bfloat16),
+            pltpu.VMEM((4 * num_pairs, seq), jnp.bfloat16),
             pltpu.VMEM((SLOTS, ROWS_PER_CHUNK, dim, seq), k_t.dtype),
             pltpu.VMEM((SLOTS, ROWS_PER_CHUNK, dim, seq), v_t.dtype),
             pltpu.SemaphoreType.DMA((2, SLOTS)),
@@ -185,7 +217,9 @@
     weights = scale_w.reshape(sources, slots, pairs, 2).transpose(0, 2, 1, 3)
     total_ctx = jnp.sum(parts * weights[..., None], axis=0)
     ctx = total_ctx / total_sum.reshape(slots, pairs, 2).transpose(1, 0, 2)[..., None]
-    ctx = ctx[:, :heads].transpose(0, 2, 1, 3).reshape(own_rows, heads * dim)
+    full = slots // 16 * 8
+    order = [h // 2 + (h % 2) * full if h < 2 * full else 2 * full + (h - 2 * full) // 2 + (h % 2) * (slots // 2 - full) for h in range(heads)]
+    ctx = ctx[:, jnp.array(order)].transpose(0, 2, 1, 3).reshape(own_rows, heads * dim)
     return ctx.astype(jnp.bfloat16)
 
 

time: 226 us -> 201 us (0.89)
  blocking collectives: 41.4 us -> 0 us
  waiting for transfers between devices: 22.6 us -> 55.3 us
  Pallas kernels: 51.4 us -> 23.9 us
  starting transfers between devices: 0.31 us -> 8.71 us
    all_to_all x1 -> x0, blocking collectives: 41.4 us -> none  [device_step(): gathered = lax.all_to_all(stats, 'sp', 0, 0, tiled=True)]
    all_to_all x0 -> x1, waiting for transfers between devices: none -> 32 us  [device_step(): gathered = lax.all_to_all(stats, 'sp', 0, 0, tiled=True)]
    pallas_call x1, Pallas kernels: 51.4 us -> 23.9 us  [attention(): pl.pallas_call(functools.partial(attention_kernel, num_pairs), out_shape=...]
    all_to_all x0 -> x1, starting transfers between devices: none -> 8.65 us  [device_step(): gathered = lax.all_to_all(stats, 'sp', 0, 0, tiled=True)]
    unnamed x14 -> x15, local copies, waits for them, and re-layouts: 6.33 us -> 6.11 us
  transfers between devices with their start and end apart: 2 -> 3, of which waited for: 1 -> 2; matrix products, arithmetic and copies ran while one was open for 20% -> 24% of each run, Pallas kernels for 23% -> 12%
where the time goes in v2:
time: 201 us
  matrix products  65.3 us (32%)
  waiting for transfers between devices  55.3 us (28%)
  local copies, waits for them, and re-layouts  24 us (12%)
  Pallas kernels  23.9 us (12%)
  between operations  14.3 us (7%)
  other arithmetic  9.45 us (5%)
  starting transfers between devices  8.71 us (4%)
    all_to_all x1, waiting for transfers between devices, device_step(): gathered = lax.all_to_all(stats, 'sp', 0, 0, tiled=True)  32 us
    pallas_call x1, Pallas kernels, attention(): pl.pallas_call(functools.partial(attention_kernel, num_pairs), out_shape=...  23.9 us
    all_gather x1, waiting for transfers between devices, device_step(): out_all = lax.all_gather(attn_out + mlp_own, 'sp', axis=0, tiled=True)  23.1 us
    dot_general x1, matrix products, device_step(): jnp.dot(normed, w_qkv, preferred_element_type=jnp.float32)  22.4 us
    dot_general x1, matrix products, device_step(): attn_out = jnp.dot(context, w_out, preferred_element_type=jnp.float32)  16.6 us
    dot_general x1, matrix products, device_step(): mlp_part = jnp.dot(activated, w_down, preferred_element_type=jnp.float32)  13.6 us
    dot_general x1, matrix products, device_step(): up_proj = jnp.dot(normed, w_up, preferred_element_type=jnp.float32)  12.7 us
    mul x2, local copies, waits for them, and re-layouts, combine(): total_ctx = jnp.sum(parts * weights[..., None], axis=0)  11.2 us
  transfers between devices with their start and end apart: 3, of which 2 were waited for; matrix products, arithmetic and copies ran while one was open for 24% of the time, Pallas kernels for 12%

profile of v2, /device:TPU:113, one launch (start us, length us, event | category | flops | bytes accessed | tf_op | source)
XLA Modules:
  0.0 200.9 jit_solution(15147393376803968093)
XLA Ops:
  7.2 1.6 copy.38
  8.9 0.3 convert_reduce_fusion
  9.1 0.5 fusion.2
  9.6 12.7 %fusion.84 = f32[128,2272]{0,1:T(8,128)S(1)} fusion(bf16[4544,2272]{1,0:T(8,128)(2,1)} %param.16, bf16[128,4544]{1,0:T(8,128)(2,1)S(1)} %copy.38, f32[4544]{0:T(1024)S(1)} %copy-done.2, f32[4544]{0:T(1024)S(1)} %copy-done.3, f32[128]{0:T(128)S(1)} %add_rsqrt_fusion, f32[128]{0:T(128)S(1)} %broadcast_multiply_fusion), kind=kOutput, calls=%fused_computation.114 | convolution fusion | flops 2646425600 | bytes 23011840 | tf_op jit(solution)/shard_map/dot_general | solution.py:240
  22.3 13.6 %fusion.18 = f32[128,4544]{1,0:T(8,128)} fusion(bf16[2272,4544]{1,0:T(8,128)(2,1)} %param.17, f32[128,2272]{0,1:T(8,128)S(1)} %fusion.84), kind=kOutput, calls=%fused_computation.34 | convolution fusion | flops 2661838848 | bytes 24137728 | tf_op jit(solution)/shard_map/dot_general | solution.py:242
  35.9 22.4 %convolution_convert_fusion = bf16[128,4672]{0,1:T(8,128)(2,1)} fusion(bf16[4544,4672]{1,0:T(8,128)(2,1)} %param.14, bf16[128,4544]{1,0:T(8,128)(2,1)S(1)} %copy.38, f32[4544]{0:T(1024)S(1)} %copy-done.2, f32[4544]{0:T(1024)S(1)} %copy-done.3, f32[128]{0:T(128)S(1)} %add_rsqrt_fusion, f32[128]{0:T(128)S(1)} %broadcast_multiply_fusion), kind=kOutput, calls=%fused_computation.1 | convolution fusion | flops 5438857216 | bytes 44855808 | tf_op jit(solution)/shard_map/dot_general | solution.py:232
  58.4 1.7 copy.39.qkv_ref
  60.1 0.3 multiply_sine_fusion
  60.4 0.2 pad_maximum_fusion
  60.6 23.9 %shard_map.130 = (bf16[128,64,1024]{2,1,0:T(8,128)(2,1)}, bf16[128,64,1024]{2,1,0:T(8,128)(2,1)}, f32[8,9,72,128]{3,2,1,0:T(8,128)S(1)}) custom-call(s32[128]{0:T(128)S(1)} %get-tuple-element.24.pos_ref, bf16[128,4672]{1,0:T(8,128)(2,1)S(1)} %copy.39.qkv_ref, f32[128,128]{1,0:T(8,128)S(1)} %get-tuple-element.25.cos_ref, ...), custom_call_target="tpu_custom_call" | custom-call | flops 2415919104 | bytes 67108864 | tf_op jit(solution)/shard_map/pallas_call | solution.py:184
  84.5 1.5 copy-done
  86.0 8.6 %all-to-all-start = ((f32[8,9,72,128]{3,2,1,0:T(8,128)}), f32[8,9,72,128]{3,2,1,0:T(8,128)}, u32[]{:S(2)}, u32[]{:S(2)}) async-start(f32[8,9,72,128]{3,2,1,0:T(8,128)} %copy-done), calls=%async_computation | async-start | bytes 5308416 | tf_op jit(solution)/shard_map/all_to_all | solution.py:237
  94.7 32.0 %all-to-all-done = f32[8,9,72,128]{3,2,1,0:T(8,128)} async-done(((f32[8,9,72,128]{3,2,1,0:T(8,128)}), f32[8,9,72,128]{3,2,1,0:T(8,128)}, u32[]{:S(2)}, u32[]{:S(2)}) %all-to-all-start) | async-done | bytes 2654240 | tf_op jit(solution)/shard_map/all_to_all | solution.py:237
  126.7 1.0 fusion.83
  127.7 0.6 copy-done.1
  128.4 1.0 slice_bitcast_fusion.1
  129.4 0.1 copy.41
  129.5 0.7 exponential_bitcast_fusion
  130.2 1.6 copy.43
  131.8 6.6 %mul.76 = f32[8,8,72,2,64]{4,3,2,1,0:T(2,128)} broadcast(f32[8,8,72,2]{3,2,1,0:T(8,128)S(1)} %copy.43), dimensions={0,1,2,3} | broadcast | bytes 2396160 | tf_op jit(solution)/shard_map/mul | solution.py:218
  138.4 4.6 %mul.77 = f32[8,8,72,128]{3,2,1,0:T(8,128)S(1)} reshape(f32[8,8,72,2,64]{4,3,2,1,0:T(2,128)} %mul.76) | data formatting | bytes 4718592 | tf_op jit(solution)/shard_map/mul | solution.py:218
  143.0 2.6 %fusion.7 = f32[8,72,128]{2,1,0:T(8,128)} fusion(f32[8,8,72,128]{3,2,1,0:T(8,128)S(1)} %mul.77, f32[8,9,72,128]{3,2,1,0:T(8,128)} %all-to-all-done), kind=kLoop, calls=%fused_computation.14 | loop fusion | flops 1105920 | bytes 5013504 | tf_op jit(solution)/shard_map/reduce_sum | solution.py:218
  145.6 1.3 reduce_sum.41
  147.0 1.3 fusion.51
  148.3 0.2 copy.45
  148.5 0.8 broadcast_divide_fusion
  149.3 1.3 gather_fusion
  150.7 0.2 convert_element_type.34
  151.0 16.6 %convolution_add_fusion = f32[16,4544]{1,0:T(8,128)} fusion(f32[16,4544]{1,0:T(8,128)} %reduce-scatter.2.cloned.1.call-done, bf16[16,4544]{1,0:T(8,128)(2,1)S(1)} %convert_element_type.34, bf16[4544,4544]{1,0:T(8,128)(2,1)} %param.15), kind=kOutput, calls=%fused_computation.2 | convolution fusion | flops 660806656 | bytes 42022912 | tf_op jit(solution)/shard_map/dot_general | solution.py:239
  167.6 23.1 %all-gather.2.cloned.1.call-done = f32[128,4544]{1,0:T(8,128)} async-done(((f32[16,4544]{1,0:T(8,128)}), f32[128,4544]{1,0:T(8,128)}) %all-gather.2.cloned.1.call-update) | async-done | bytes 2326544 | tf_op jit(solution)/shard_map/all_gather | solution.py:244
  190.8 1.9 fusion.6
  192.6 1.4 copy.47
  (23 shorter events, 0.4 us)
Async XLA Ops:
  7.2 143.8 %reduce-scatter.2.cloned.1.call-start = ((), (), s32[]{:S(2)}) async-start(), calls=%async_computation.2 | async-start | bytes 2654208 | tf_op jit(solution)/shard_map/reduce_scatter | solution.py:243
  8.8 0.8 copy-start.2
  8.8 0.8 copy-start.3
  58.4 1.8 copy-start.5
  84.5 1.5 copy-start
  86.0 8.7 %copy-start.4 = (s32[71]{0:T(128)S(1)}, s32[71]{0:T(128)}, u32[]{:S(2)}) copy-start(s32[71]{0:T(128)} %constant.94) | copy-start | bytes 856
  86.0 40.7 %all-to-all-start = ((f32[8,9,72,128]{3,2,1,0:T(8,128)}), f32[8,9,72,128]{3,2,1,0:T(8,128)}, u32[]{:S(2)}, u32[]{:S(2)}) async-start(f32[8,9,72,128]{3,2,1,0:T(8,128)} %copy-done), calls=%async_computation | async-start | bytes 5308416 | tf_op jit(solution)/shard_map/all_to_all | solution.py:237
  94.7 96.1 %all-gather.2.cloned.1.call-start = ((), (), s32[]{:S(2)}) async-start(), calls=%async_computation.3 | async-start | bytes 2654208 | tf_op jit(solution)/shard_map/all_gather | solution.py:244
  127.7 0.6 copy-start.1
Sparse Core Ops, SparseCore 0:
  36.0 30.1 reduce-scatter.1
  167.8 22.9 all-gather.1
